TPU v7x, 512 devices: a 4x2x32 block of a 4x8x32 slice. The times are simulated.
512 devices in a mesh: groups: 2 (over y), seq: 32 (over z), head: 4 (over x), rep: 2 (over core).
Axes of the slice: x: 4, y: 2, z: 32, core: 2. Of those that a mesh axis runs over, the one named last changes fastest.
The devices are a block of a 4x8x32 slice.
Arguments:
- prefix_x: bfloat16 [8192, 8192], P(('groups', 'seq'), ('head', 'rep')), parts along dimension 0, may hold values from -6 to 6
- prefix_b: bfloat16 [8192, 8, 256], P(('groups', 'seq'), ('head', 'rep')), parts along dimension 0, may hold values from -0.09375 to 0.09375
- prefix_c: bfloat16 [8192, 8, 256], P(('groups', 'seq'), ('head', 'rep')), parts along dimension 0, may hold values from -0.375 to 0.375
- prefix_decay: float32 [8192, 128], P(('groups', 'seq'), ('head', 'rep')), parts along dimension 0, may hold values from 0 to 1.5, as said below
- bypass_weight: float32 [128], replicated, may hold values from 0.1 to 1.9
- prefix_key_rows: bfloat16 [8192, 4, 128], P(('groups', 'seq'), 'head'), parts along dimension 0, may hold values from -8 to 8
- prefix_values: bfloat16 [8192, 4, 128], P(('groups', 'seq'), 'head'), parts along dimension 0, may hold values from -6 to 6
- cand_x: bfloat16 [128, 32, 8192], P(('groups', 'seq', 'rep'), None, 'head'), parts along dimension 0, may hold values from -6 to 6
- cand_b: bfloat16 [128, 32, 8, 256], P(('groups', 'seq', 'rep'), None, 'head'), parts along dimension 0, may hold values from -0.09375 to 0.09375
- cand_c: bfloat16 [128, 32, 8, 256], P(('groups', 'seq', 'rep'), None, 'head'), parts along dimension 0, may hold values from -0.375 to 0.375
- cand_decay: float32 [128, 32, 128], P(('groups', 'seq', 'rep'), None, 'head'), parts along dimension 0, may hold values from 0 to 1.5, as said below
- cand_queries: bfloat16 [128, 32, 32, 128], P(('groups', 'seq', 'rep'), None, 'head'), parts along dimension 0, may hold values from -8 to 8
- cand_keys: bfloat16 [128, 32, 4, 128], P(('groups', 'seq', 'rep'), None, 'head'), parts along dimension 0, may hold values from -16 to 16
- cand_values: bfloat16 [128, 32, 4, 128], P(('groups', 'seq', 'rep'), None, 'head'), parts along dimension 0, may hold values from -6 to 6
- cand_length: int32 [128], P(('groups', 'seq', 'rep')), parts along dimension 0, may hold values from 16 to 32
Outputs:
- prefix_out: bfloat16 [8192, 8192], P(('groups', 'seq'), ('head', 'rep')), parts along dimension 0
- cand_ssm: bfloat16 [128, 32, 8192], P(('groups', 'seq', 'rep'), None, 'head'), parts along dimension 0
- cand_attn: bfloat16 [128, 32, 32, 128], P(('groups', 'seq', 'rep'), None, 'head'), parts along dimension 0
There are 2 independent parts, one for each index of `groups`. A program takes and returns all parts, laid end to end along the dimension named above; an argument that names none is the same for every part. Nothing has to cross between parts.
Inputs may be any that keep to these rules, and one draw needn't show every extreme that they name: `prefix_decay`: positive. `cand_decay`: positive.
All inputs are finite; a program needn't handle non-finite values.
Results may differ from a plain program's by a relative error of at most 0.008.
Values may be sent and summed in bfloat16 or wider, within the bound.
A program may use at most 128 MiB of HBM per device.

v0:
```python
import math
import jax
import jax.numpy as jnp
from jax import lax
from jax.sharding import PartitionSpec as P

EPSILON = 1e-06
FLOOR = -1e30


def entering(part, axis, combine, identity):
    place = lax.axis_index(axis)
    gathered = jax.tree.map(lambda a: lax.all_gather(a, axis), part)
    state = jax.tree.map(lambda a, e: jnp.zeros_like(a) + jnp.asarray(e, a.dtype), part, identity)

    def one(hop, state):
        return combine(
            state, jax.tree.map(lambda a: lax.dynamic_index_in_dim(a, hop, 0, False), gathered)
        )

    return lax.fori_loop(0, place, one, state)


def copy_for_each(x, axis):
    count = lax.axis_size(axis)
    return lax.all_to_all(jnp.broadcast_to(x[None], (count, *x.shape)), axis, 0, 0, tiled=True)


def combined_pairwise(pieces, combine):
    while len(jax.tree.leaves(pieces)[0]) > 1:
        pieces = jax.vmap(combine)(*(pieces[side::2] for side in (0, 1)))
    return pieces[0]


def entering_2(x, axis, combine, identity):
    count, position = (lax.axis_size(axis), lax.axis_index(axis))
    passed = jnp.arange(count) > position

    def kept(part, zero, own):
        part = jnp.where(
            passed.reshape(-1, *(1 for _ in own.shape)), part, jnp.asarray(zero, own.dtype)
        )
        return part[::-1]

    pieces = copy_for_each(x, axis)
    return combined_pairwise(kept(pieces, identity, x), combine)


def laid_out(tiles, dim):
    tiles = jnp.moveaxis(tiles, 0, dim)
    lengths = tiles.shape
    return tiles.reshape(*lengths[:dim], lengths[dim] * lengths[dim + 1], *lengths[dim + 2 :])


def gather_directly(x, axis, dim):
    return laid_out(copy_for_each(x, axis), dim)


def sent_together(arrays, axis, dim, along):
    widths = [a.shape[along] for a in arrays]
    both = jnp.concatenate(arrays, axis=along)
    result = lax.all_gather(both, axis, axis=dim, tiled=True)
    return tuple(jnp.split(result, [sum(widths[:k]) for k in range(1, len(widths))], axis=along))


def summarize(x, bmat, decay):
    length, groups, state = bmat.shape
    heads = decay.shape[1]
    per_group = heads // groups
    width = x.shape[1] // heads
    cum = jnp.cumsum(decay, axis=0)
    total = jnp.exp(-cum[-1])
    weights = jnp.exp(cum[-1][None, :] - cum)
    inputs = x.reshape(length, heads, width)
    weighted = (inputs.astype(jnp.float32) * weights[:, :, None]).astype(jnp.bfloat16)
    weighted = weighted.reshape(length, groups, per_group, width)
    local = jnp.einsum("sgn,sgkp->gknp", bmat, weighted, preferred_element_type=jnp.float32)
    return (cum, total, local.reshape(heads, state, width))


def emit(x, bmat, cmat, cum, skip, start):
    length, groups, state = bmat.shape
    heads = cum.shape[1]
    per_group = heads // groups
    width = x.shape[1] // heads
    inputs = x.reshape(length, heads, width)
    gram = jnp.einsum("tgn,sgn->gts", cmat, bmat, preferred_element_type=jnp.float32)
    span = math.gcd(per_group, 4)
    count = heads // span
    causal = lax.broadcasted_iota(jnp.int32, (length, length), 0) >= lax.broadcasted_iota(
        jnp.int32, (length, length), 1
    )
    cum_sets = cum.T.reshape(count, span, length)
    input_sets = inputs.reshape(length, count, span, width).transpose(1, 0, 2, 3)

    def one_set(piece):
        index, cum_set, input_set = piece
        gram_set = lax.dynamic_index_in_dim(gram, index * span // per_group, 0, keepdims=False)
        gap = cum_set[:, :, None] - cum_set[:, None, :]
        state_mixing = jnp.where(causal, jnp.exp(-jnp.where(causal, gap, 0.0)), 0.0) * gram_set
        return jnp.einsum(
            "hts,shp->thp",
            state_mixing.astype(jnp.bfloat16),
            input_set,
            preferred_element_type=jnp.float32,
        )

    intra = lax.map(one_set, (jnp.arange(count, dtype=jnp.int32), cum_sets, input_sets))
    intra = intra.transpose(1, 0, 2, 3).reshape(length, heads, width)
    start_set = start.reshape(groups, per_group, state, width)
    carried = jnp.einsum("tgn,gknp->tgkp", cmat.astype(jnp.float32), start_set)
    carried = carried.reshape(length, heads, width)
    result = (
        intra
        + jnp.exp(-cum)[:, :, None] * carried
        + skip[None, :, None] * inputs.astype(jnp.float32)
    )
    return result.reshape(length, heads * width).astype(jnp.bfloat16)


def chain_step(earlier, later):
    return (earlier[0] * later[0], later[0][:, None, None] * earlier[1] + later[1])


def elementwise_product(earlier, later):
    return earlier * later


def blend(carry, scores, values):
    top, mass, acc = carry
    new_top = jnp.maximum(top, scores.max(-1))
    fade = jnp.exp(top - new_top)
    weights = jnp.exp(scores - new_top[..., None])
    mass = mass * fade + weights.sum(-1)
    acc = acc * fade[..., None] + jnp.einsum(
        "ctkqs,skd->ctkqd", weights.astype(jnp.bfloat16), values, preferred_element_type=jnp.float32
    )
    return (new_top, mass, acc)


def join(first, second):
    top = jnp.maximum(first[0], second[0])
    one = jnp.exp(first[0] - top)
    two = jnp.exp(second[0] - top)
    return (
        top,
        first[1] * one + second[1] * two,
        first[2] * one[..., None] + second[2] * two[..., None],
    )


def key_folder(query_set, scale, carry, piece):
    keys, values = piece
    rows = keys.shape[0]
    step = math.gcd(rows, 1024)

    def one_block(inner, index):
        key_block = lax.dynamic_slice_in_dim(keys, index * step, step, 0)
        value_block = lax.dynamic_slice_in_dim(values, index * step, step, 0)
        scores = (
            jnp.einsum("ctkqd,skd->ctkqs", query_set, key_block, preferred_element_type=jnp.float32)
            * scale
        )
        return (blend(inner, scores, value_block), None)

    carry, unused = lax.scan(one_block, carry, jnp.arange(rows // step, dtype=jnp.int32))
    return carry


def empty_softmax(count, steps, kv_local, per_kv, dim):
    shape = (count, steps, kv_local, per_kv)
    return (
        jnp.full(shape, FLOOR, jnp.float32),
        jnp.zeros(shape, jnp.float32),
        jnp.zeros(shape + (dim,), jnp.float32),
    )


def on_device(
    prefix_x,
    prefix_b,
    prefix_c,
    prefix_decay,
    bypass_weight,
    prefix_key_rows,
    prefix_values,
    cand_x,
    cand_b,
    cand_c,
    cand_decay,
    cand_queries,
    cand_keys,
    cand_values,
    cand_length,
):
    local_heads = prefix_decay.shape[1]
    spread = lax.axis_size("rep")
    offset = (lax.axis_index("head") * spread + lax.axis_index("rep")) * local_heads
    skip_local = lax.dynamic_slice_in_dim(bypass_weight, offset, local_heads)
    cum, total, local = summarize(prefix_x, prefix_b, prefix_decay)
    identity = (jnp.ones_like(total), jnp.zeros_like(local))
    carried_in = entering((total, local), "seq", chain_step, identity)[1]
    prefix_out = emit(prefix_x, prefix_b, prefix_c, cum, skip_local, carried_in)
    beyond = entering_2(total, "seq", elementwise_product, jnp.ones_like(total))
    final = lax.psum(beyond[:, None, None] * local, "seq")
    heads_final = gather_directly(final, "rep", 0)
    cand_heads = cand_decay.shape[2]
    cand_skip = lax.dynamic_slice_in_dim(
        bypass_weight, lax.axis_index("head") * cand_heads, cand_heads
    )
    steps = cand_x.shape[1]
    valid = lax.broadcasted_iota(jnp.int32, (steps,), 0) < cand_length[0]
    cand_cum = jnp.cumsum(cand_decay[0], axis=0)
    cand_out = emit(cand_x[0], cand_b[0], cand_c[0], cand_cum, cand_skip, heads_final)
    cand_ssm = jnp.where(valid[:, None], cand_out, jnp.zeros((), jnp.bfloat16))[None]
    kv_local = prefix_key_rows.shape[1]
    dim = prefix_key_rows.shape[2]
    per_kv = cand_queries.shape[2] // kv_local
    scale = dim ** (-0.5)
    query = cand_queries[0].reshape(steps, kv_local, per_kv, dim)
    init = empty_softmax(1, steps, kv_local, per_kv, dim)
    part = key_folder(
        query[None], scale, init, sent_together((prefix_key_rows, prefix_values), "seq", 0, 1)
    )
    part = (part[0][0], part[1][0], part[2][0])
    own_scores = (
        jnp.einsum("tkqd,skd->tkqs", query, cand_keys[0], preferred_element_type=jnp.float32)
        * scale
    )
    visible = lax.broadcasted_iota(jnp.int32, (steps, 1, 1, steps), 0) >= lax.broadcasted_iota(
        jnp.int32, (steps, 1, 1, steps), 3
    )
    own_scores = jnp.where(visible, own_scores, FLOOR)
    own_top = own_scores.max(-1)
    own_weights = jnp.exp(own_scores - own_top[..., None])
    own_acc = jnp.einsum(
        "tkqs,skd->tkqd",
        own_weights.astype(jnp.bfloat16),
        cand_values[0],
        preferred_element_type=jnp.float32,
    )
    top, mass, acc = join(part, (own_top, own_weights.sum(-1), own_acc))
    mixed = acc / mass[..., None]
    mixed = mixed * lax.rsqrt(jnp.mean(mixed * mixed, axis=-1, keepdims=True) + EPSILON)
    mixed = mixed.reshape(steps, kv_local * per_kv, dim)
    cand_attn = jnp.where(valid[:, None, None], mixed, 0.0).astype(jnp.bfloat16)[None]
    return (prefix_out, cand_ssm, cand_attn)


def solution(mesh):
    placed = (
        P(("groups", "seq"), ("head", "rep")),
        P(("groups", "seq"), ("head", "rep"), None),
        P(("groups", "seq"), ("head", "rep"), None),
        P(("groups", "seq"), ("head", "rep")),
        P(),
        P(("groups", "seq"), "head", None),
        P(("groups", "seq"), "head", None),
        P(("groups", "seq", "rep"), None, "head"),
        P(("groups", "seq", "rep"), None, "head", None),
        P(("groups", "seq", "rep"), None, "head", None),
        P(("groups", "seq", "rep"), None, "head"),
        P(("groups", "seq", "rep"), None, "head", None),
        P(("groups", "seq", "rep"), None, "head", None),
        P(("groups", "seq", "rep"), None, "head", None),
        P(("groups", "seq", "rep")),
    )
    return jax.shard_map(
        on_device,
        mesh=mesh,
        in_specs=placed,
        out_specs=(
            P(("groups", "seq"), ("head", "rep")),
            P(("groups", "seq", "rep"), None, "head"),
            P(("groups", "seq", "rep"), None, "head", None),
        ),
        check_vma=False,
    )
```

profile of v0, /device:TPU:2016, one launch (start us, length us, event | category | flops | bytes accessed | tf_op | source)
XLA Modules:
  0.0 707.2 jit_solution(14934478910430227610)
XLA Ops:
  7.3 1.4 pad_maximum_fusion
  10.3 5.2 all-to-all-start
  16.9 17.7 %all-to-all-done = f32[32,1,16]{2,1,0:T(1,128)S(1)} async-done(((f32[32,1,16]{2,1,0:T(1,128)}), f32[32,1,16]{2,1,0:T(1,128)S(1)}, u32[]{:S(2)}, u32[]{:S(2)}) %all-to-all-start) | async-done | bytes 2080 | tf_op jit(solution)/shard_map/all_to_all | solution.py:26
  40.7 13.2 %while.56 = (s32[]{:T(128)}, f32[8,32,4,64]{3,1,2,0:T(8,128)S(1)}, bf16[8,32,4,64]{3,2,0,1:T(4,128)(2,1)S(1)}, f32[8,4,32]{2,1,0:T(4,128)S(1)}, s32[8]{0:T(128)S...) while((s32[]{:T(128)}, f32[8,32,4,64]{3,1,2,0:T(8,128)S(1)}, ...), condition=%wide.region_7.8_spmd.clone.clone, body=%wide.region_6.7_spmd.clone.clone.sunk | while | flops 549909 | bytes 166245 | solution.py:108
  54.7 53.0 %all-gather = f32[32,1,16]{2,1,0:T(1,128)S(1)} all-gather(f32[1,1,16]{2,1,0:T(1,128)S(1)} %get-tuple-element.433), channel_id=1, replica_groups=mesh['groups'=2,'seq'=32,'head'=4,'rep'=2] {'seq'}, dimensions={0}, use_global_device_ids=true | all-gather | bytes 2112 | tf_op jit(solution)/shard_map/all_gather | solution.py:13
  107.8 3.9 while.55
  111.7 133.8 %all-reduce.1 = bf16[16,256,64]{1,2,0:T(8,128)(2,1)S(1)} all-reduce(f32[16,256,64]{1,2,0:T(8,128)S(1)} %get-tuple-element.436), channel_id=1, replica_groups=mesh['groups'=2,'seq'=32,'head'=4,'rep'=2] {'seq'}, use_global_device_ids=true, to_apply=%region_8.9 | all-reduce | flops 262144 | bytes 1572864 | tf_op jit(solution)/shard_map/psum | solution.py:205
  245.6 4.6 all_to_all.14
  252.1 1.7 fusion.72
  253.8 9.7 %while.57 = (s32[]{:T(128)}, f32[1,32,1,8]{1,3,2,0:T(8,128)S(1)}, f32[1,32,1,8]{1,3,2,0:T(8,128)S(1)}, f32[1,32,1,8,128]{4,1,3,0,2:T(8,128)S(1)}, s32[4]{0:T(128...) while((s32[]{:T(128)}, f32[1,32,1,8]{1,3,2,0:T(8,128)S(1)}, ...), condition=%wide.region_12.13_spmd.clone, body=%wide.region_9.12_spmd.clone.sunk | while | flops 135890432 | bytes 4020427 | solution.py:166
  264.8 251.0 %all-gather.4.cloned.1.call-done = f32[32,16,256,64]{2,3,1,0:T(8,128)} async-done(((f32[1,16,256,64]{2,3,1,0:T(8,128)}), f32[32,16,256,64]{2,3,1,0:T(8,128)}) %all-gather.4.cloned.1.call-update) | async-done | bytes 33554448 | tf_op jit(solution)/shard_map/all_gather | solution.py:13
  515.9 1.5 broadcast_in_dim.147
  517.4 179.7 %while.54 = (s32[]{:T(128)}, f32[16,256,64]{2,1,0:T(8,128)}, s32[]{:T(128)}, f32[32,16]{1,0:T(8,128)S(1)}, f32[32,16,256,64]{2,3,1,0:T(8,128)}, /*index=5*/s32[]{:T(128)}, s32[]{:T(128)}, s32[]{:T(128)}) while((s32[]{:T(128)}, f32[16,256,64]{2,1,0:T(8,128)}, s32[]{:T(128)}, f32[32,16]{1,0:T(8,128)S(1)}, f32[32,16,256,64]{2,3,1,0:T(8,128)}, ...), condition=%wide.region_4.5_spmd, body=%wide.region_3.4_spmd.sunk | while | flops 524293 | bytes 7356799 | solution.py:21
  518.0 1.3 constant_dynamic-slice_fusion.4
  520.0 3.2 bitcast_add_fusion.4
  525.8 3.2 bitcast_add_fusion.4
  529.6 1.3 constant_dynamic-slice_fusion.4
  531.6 3.2 bitcast_add_fusion.4
  535.4 1.3 constant_dynamic-slice_fusion.4
  537.4 3.2 bitcast_add_fusion.4
  543.2 3.2 bitcast_add_fusion.4
  548.9 3.2 bitcast_add_fusion.4
  554.7 3.2 bitcast_add_fusion.4
  560.5 3.2 bitcast_add_fusion.4
  566.3 3.2 bitcast_add_fusion.4
  572.1 3.2 bitcast_add_fusion.4
  577.9 3.2 bitcast_add_fusion.4
  583.7 3.2 bitcast_add_fusion.4
  589.5 3.2 bitcast_add_fusion.4
  595.3 3.2 bitcast_add_fusion.4
  601.1 3.2 bitcast_add_fusion.4
  606.9 3.2 bitcast_add_fusion.4
  612.7 3.2 bitcast_add_fusion.4
  618.5 3.2 bitcast_add_fusion.4
  624.3 3.2 bitcast_add_fusion.4
  630.1 3.2 bitcast_add_fusion.4
  635.9 3.2 bitcast_add_fusion.4
  641.7 3.2 bitcast_add_fusion.4
  647.5 3.2 bitcast_add_fusion.4
  653.3 3.2 bitcast_add_fusion.4
  659.1 3.2 bitcast_add_fusion.4
  664.9 3.2 bitcast_add_fusion.4
  670.7 3.2 bitcast_add_fusion.4
  676.5 3.2 bitcast_add_fusion.4
  682.3 3.2 bitcast_add_fusion.4
  688.1 3.2 bitcast_add_fusion.4
  693.9 3.2 bitcast_add_fusion.4
  697.1 2.1 fusion.51
  (406 shorter events, 106.2 us)
Async XLA Ops:
  7.2 27.8 %copy-start = (bf16[128,1,256]{2,0,1:T(8,128)(2,1)S(1)}, bf16[128,1,256]{2,0,1:T(8,128)(2,1)}, u32[]{:S(2)}) copy-start(bf16[128,1,256]{2,0,1:T(8,128)(2,1)} %param.24) | copy-start | bytes 196612
  7.2 244.9 %all-gather.6.cloned.1.call-start = ((), (), s32[]{:S(2)}) async-start(), calls=%async_computation.3 | async-start | bytes 2162688 | tf_op jit(solution)/shard_map/all_gather | solution.py:62
  10.3 24.3 %all-to-all-start = ((f32[32,1,16]{2,1,0:T(1,128)}), f32[32,1,16]{2,1,0:T(1,128)S(1)}, u32[]{:S(2)}, u32[]{:S(2)}) async-start(f32[32,1,16]{2,1,0:T(1,128)} %broadcast_in_dim.151), calls=%async_computation | async-start | bytes 32768 | tf_op jit(solution)/shard_map/all_to_all | solution.py:26
  15.5 500.4 %all-gather.4.cloned.1.call-start = ((), (), s32[]{:S(2)}) async-start(), calls=%async_computation.2 | async-start | bytes 34603008 | tf_op jit(solution)/shard_map/all_gather | solution.py:13
  16.8 20.1 %copy-start.15 = (f32[128]{0:T(128)S(1)}, f32[128]{0:T(128)}, u32[]{:S(2)}) copy-start(f32[128]{0:T(128)} %param.27) | copy-start | bytes 1540
  16.8 21.8 %copy-start.10 = (f32[1,32,32]{2,1,0:T(8,128)S(1)}, f32[1,32,32]{2,1,0:T(8,128)}, u32[]{:S(2)}) copy-start(f32[1,32,32]{2,1,0:T(8,128)} %param.33) | copy-start | bytes 12292
  16.9 21.9 %copy-start.3 = (bf16[1,32,8,128]{3,2,1,0:T(8,128)(2,1)S(1)}, bf16[1,32,8,128]{3,2,1,0:T(8,128)(2,1)}, u32[]{:S(2)}) copy-start(bf16[1,32,8,128]{3,2,1,0:T(8,128)(2,1)} %param.34) | copy-start | bytes 196612
  16.9 22.0 %copy-start.13 = (bf16[1,32,1,128]{3,1,2,0:T(8,128)(2,1)S(1)}, bf16[1,32,1,128]{3,1,2,0:T(8,128)(2,1)}, u32[]{:S(2)}) copy-start(bf16[1,32,1,128]{3,1,2,0:T(8,128)(2,1)} %param.35) | copy-start | bytes 24580
  34.9 5.0 copy-start.2
  36.2 4.4 copy-start.5
  36.2 4.4 copy-start.7
  40.6 67.1 %copy-start.4 = (bf16[128,1,256]{2,0,1:T(8,128)(2,1)S(1)}, bf16[128,1,256]{2,0,1:T(8,128)(2,1)}, u32[]{:S(2)}) copy-start(bf16[128,1,256]{2,0,1:T(8,128)(2,1)} %param.25) | copy-start | bytes 196612
  250.2 1.1 copy-start.6
  253.8 9.8 %copy-start.9 = (f32[32,8]{0,1:T(8,128)S(1)}, f32[32,8]{0,1:T(8,128)}, u32[]{:S(2)}) copy-start(f32[32,8]{0,1:T(8,128)} %get-tuple-element.429) | copy-start | bytes 3076
  253.8 10.0 %copy-start.14 = (bf16[1,32,1,128]{3,1,2,0:T(8,128)(2,1)S(1)}, bf16[1,32,1,128]{3,1,2,0:T(8,128)(2,1)}, u32[]{:S(2)}) copy-start(bf16[1,32,1,128]{3,1,2,0:T(8,128)(2,1)} %param.36) | copy-start | bytes 24580
  519.9 3.3 copy-start.12
  525.7 3.3 copy-start.12
  531.5 3.3 copy-start.12
  537.3 3.3 copy-start.12
  543.1 3.3 copy-start.12
  548.9 3.3 copy-start.12
  554.7 3.3 copy-start.12
  560.5 3.3 copy-start.12
  566.3 3.3 copy-start.12
  572.1 3.3 copy-start.12
  577.9 3.3 copy-start.12
  583.7 3.3 copy-start.12
  589.5 3.3 copy-start.12
  595.3 3.3 copy-start.12
  601.1 3.3 copy-start.12
  606.9 3.3 copy-start.12
  612.7 3.3 copy-start.12
  618.5 3.3 copy-start.12
  624.3 3.3 copy-start.12
  630.1 3.3 copy-start.12
  635.9 3.3 copy-start.12
  641.7 3.3 copy-start.12
  647.5 3.3 copy-start.12
  653.3 3.3 copy-start.12
  659.1 3.3 copy-start.12
  664.9 3.3 copy-start.12
  670.7 3.3 copy-start.12
  676.5 3.3 copy-start.12
  682.3 3.3 copy-start.12
  688.1 3.3 copy-start.12
  693.9 3.3 copy-start.12
  697.1 2.2 copy-start.1
  697.1 2.2 copy-start.8
  (31 other events, 18.8 us)
Sparse Core Ops, SparseCore 0:
  10.7 119.5 all-gather.5
  132.4 383.4 all-gather.3
where the time goes:
time: 710 us; the launch traced here: 707 us
  waiting for transfers between devices  269 us (38%)
  blocking collectives  191 us (27%)
  other arithmetic  106 us (15%)
  local copies, waits for them, and re-layouts  97.6 us (14%)
  between operations  15.1 us (2%)
  matrix products  13.4 us (2%)
  loops' own time  9.57 us (1%)
    all_gather x1, waiting for transfers between devices, entering(): gathered = jax.tree.map(lambda a: lax.all_gather(a, axis), part)  251 us
    psum x1, blocking collectives, on_device(): final = lax.psum(beyond[:, None, None] * local, 'seq')  134 us
    add x31, other arithmetic, chain_step(): later[0][:, None, None] * earlier[1] + later[1]  100 us
    dynamic_slice x62, local copies, waits for them, and re-layouts, one(): lax.dynamic_index_in_dim(a, hop, 0, False)  59.4 us
    all_gather x1, blocking collectives, entering(): gathered = jax.tree.map(lambda a: lax.all_gather(a, axis), part)  53 us
    while x128, local copies, waits for them, and re-layouts  19 us
    all_to_all x1, waiting for transfers between devices, copy_for_each(): lax.all_to_all(jnp.broadcast_to(x[None], (count, *x.shape)), axis, 0, 0,...  17.7 us
  transfers between devices with their start and end apart: 3, of which 2 were waited for; matrix products, arithmetic and copies ran while one was open for 5% of the time, Pallas kernels for 0%

commit v1 on v0

--- a/solution.py
+++ b/solution.py
@@ -202,7 +202,7 @@
     carried_in = entering((total, local), "seq", chain_step, identity)[1]
     prefix_out = emit(prefix_x, prefix_b, prefix_c, cum, skip_local, carried_in)
     beyond = entering_2(total, "seq", elementwise_product, jnp.ones_like(total))
-    final = lax.psum(beyond[:, None, None] * local, "seq")
+    final = jnp.sum(lax.all_gather(beyond[:, None, None] * local, "seq"), axis=0)
     heads_final = gather_directly(final, "rep", 0)
     cand_heads = cand_decay.shape[2]
     cand_skip = lax.dynamic_slice_in_dim(

time: 710 us -> 1080 us (1.52)
  waiting for transfers between devices: 269 us -> 757 us
  blocking collectives: 191 us -> 57.5 us
  other arithmetic: 106 us -> 117 us
    all_gather x0 -> x1, waiting for transfers between devices: none -> 361 us  [on_device(): lax.all_gather(beyond[:, None, None] * local, 'seq')]
    psum x1 -> x0, blocking collectives: 134 us -> none  [on_device(): final = lax.psum(beyond[:, None, None] * local, 'seq')]
    all_gather x1, waiting for transfers between devices: 251 us -> 361 us  [entering(): gathered = jax.tree.map(lambda a: lax.all_gather(a, axis), part)]
    all_gather x1, waiting for transfers between devices: 0.01 us -> 17.4 us  [sent_together(): result = lax.all_gather(both, axis, axis=dim, tiled=True)]
    reduce_sum x0 -> x1, other arithmetic: none -> 12 us  [on_device(): jnp.sum(lax.all_gather(beyond[:, None, None] * local, 'seq'), axis=0)]
  transfers between devices with their start and end apart: 3 -> 4, of which waited for: 2 -> 4; matrix products, arithmetic and copies ran while one was open for 5% -> 4% of each run, Pallas kernels for 0% -> 0%
where the time goes in v1:
time: 1080 us; the launch traced here: 1070 us
  waiting for transfers between devices  757 us (70%)
  other arithmetic  117 us (11%)
  local copies, waits for them, and re-layouts  99.1 us (9%)
  blocking collectives  57.5 us (5%)
  between operations  14.8 us (1%)
  matrix products  13.8 us (1%)
    all_gather x1, waiting for transfers between devices, entering(): gathered = jax.tree.map(lambda a: lax.all_gather(a, axis), part)  361 us
    all_gather x1, waiting for transfers between devices, on_device(): lax.all_gather(beyond[:, None, None] * local, 'seq')  361 us
    add x31, other arithmetic, chain_step(): later[0][:, None, None] * earlier[1] + later[1]  99.7 us
    dynamic_slice x62, local copies, waits for them, and re-layouts, one(): lax.dynamic_index_in_dim(a, hop, 0, False)  59.4 us
    all_gather x1, blocking collectives, entering(): gathered = jax.tree.map(lambda a: lax.all_gather(a, axis), part)  52.9 us
  transfers between devices with their start and end apart: 4, of which 4 were waited for; matrix products, arithmetic and copies ran while one was open for 4% of the time, Pallas kernels for 0%

profile of v1, /device:TPU:2016, one launch (start us, length us, event | category | flops | bytes accessed | tf_op | source)
XLA Modules:
  0.0 1074.3 jit_solution(11174128698635868656)
XLA Ops:
  7.3 1.4 pad_maximum_fusion
  10.3 5.2 all-to-all-start
  16.9 17.8 %all-to-all-done = f32[32,1,16]{2,1,0:T(1,128)S(1)} async-done(((f32[32,1,16]{2,1,0:T(1,128)}), f32[32,1,16]{2,1,0:T(1,128)S(1)}, u32[]{:S(2)}, u32[]{:S(2)}) %all-to-all-start) | async-done | bytes 2080 | tf_op jit(solution)/shard_map/all_to_all | solution.py:26
  35.0 1.6 broadcast_multiply_fusion
  41.5 13.2 %while.56 = (s32[]{:T(128)}, f32[8,32,4,64]{3,1,2,0:T(8,128)S(1)}, bf16[8,32,4,64]{3,2,0,1:T(4,128)(2,1)S(1)}, f32[8,4,32]{2,1,0:T(4,128)S(1)}, s32[8]{0:T(128)S...) while((s32[]{:T(128)}, f32[8,32,4,64]{3,1,2,0:T(8,128)S(1)}, ...), condition=%wide.region_7.8_spmd.clone.clone, body=%wide.region_6.7_spmd.clone.clone.sunk | while | flops 549909 | bytes 166245 | solution.py:108
  56.1 52.9 %all-gather = f32[32,1,16]{2,1,0:T(1,128)S(1)} all-gather(f32[1,1,16]{2,1,0:T(1,128)S(1)} %get-tuple-element.433), channel_id=1, replica_groups=mesh['groups'=2,'seq'=32,'head'=4,'rep'=2] {'seq'}, dimensions={0}, use_global_device_ids=true | all-gather | bytes 2112 | tf_op jit(solution)/shard_map/all_gather | solution.py:13
  109.2 3.9 while.55
  113.1 17.4 %all-gather.9.cloned.1.call-done = bf16[4096,2,128]{2,0,1:T(8,128)(2,1)} async-done(((bf16[128,2,128]{2,0,1:T(8,128)(2,1)}), bf16[4096,2,128]{2,0,1:T(8,128)(2,1)}) %all-gather.9.cloned.1.call-update) | async-done | bytes 2097168 | tf_op jit(solution)/shard_map/all_gather | solution.py:62
  130.4 1.7 fusion.71
  132.1 9.7 while.57
  143.2 360.5 %all-gather.7.cloned.1.call-done = f32[32,16,256,64]{2,3,1,0:T(8,128)} async-done(((f32[1,16,256,64]{2,3,1,0:T(8,128)}), f32[32,16,256,64]{2,3,1,0:T(8,128)}) %all-gather.7.cloned.1.call-update) | async-done | bytes 33554448 | tf_op jit(solution)/shard_map/all_gather | solution.py:205
  503.7 12.0 %reduce_sum.38 = bf16[16,256,64]{1,2,0:T(8,128)(2,1)S(1)} reduce(f32[32,16,256,64]{2,3,1,0:T(8,128)} %all-gather.7.cloned.1.call-done, f32[]{:T(128)} %constant.160.clone.1), dimensions={0}, to_apply=%region_8.9 | reduce | flops 8126464 | bytes 34078724 | tf_op jit(solution)/shard_map/reduce_sum | solution.py:205
  515.9 4.6 all_to_all.14
  522.2 360.8 %all-gather.5.cloned.1.call-done = f32[32,16,256,64]{2,3,1,0:T(8,128)} async-done(((f32[1,16,256,64]{2,3,1,0:T(8,128)}), f32[32,16,256,64]{2,3,1,0:T(8,128)}) %all-gather.5.cloned.1.call-update) | async-done | bytes 33554448 | tf_op jit(solution)/shard_map/all_gather | solution.py:13
  883.1 1.5 broadcast_in_dim.147
  884.6 179.1 %while.54 = (s32[]{:T(128)}, f32[16,256,64]{2,1,0:T(8,128)}, s32[]{:T(128)}, f32[32,16]{1,0:T(8,128)S(1)}, f32[32,16,256,64]{2,3,1,0:T(8,128)}, /*index=5*/s32[]{:T(128)}, s32[]{:T(128)}, s32[]{:T(128)}) while((s32[]{:T(128)}, f32[16,256,64]{2,1,0:T(8,128)}, s32[]{:T(128)}, f32[32,16]{1,0:T(8,128)S(1)}, f32[32,16,256,64]{2,3,1,0:T(8,128)}, ...), condition=%wide.region_4.5_spmd, body=%wide.region_3.4_spmd.sunk | while | flops 524293 | bytes 7356799 | solution.py:21
  887.1 3.2 bitcast_add_fusion.4
  892.9 3.2 bitcast_add_fusion.4
  898.7 3.2 bitcast_add_fusion.4
  904.5 3.2 bitcast_add_fusion.4
  910.2 3.2 bitcast_add_fusion.4
  916.0 3.2 bitcast_add_fusion.4
  921.8 3.2 bitcast_add_fusion.4
  927.6 3.2 bitcast_add_fusion.4
  933.3 3.2 bitcast_add_fusion.4
  939.1 3.2 bitcast_add_fusion.4
  944.9 3.2 bitcast_add_fusion.4
  950.7 3.2 bitcast_add_fusion.4
  956.5 3.2 bitcast_add_fusion.4
  962.2 3.2 bitcast_add_fusion.4
  968.0 3.2 bitcast_add_fusion.4
  973.8 3.2 bitcast_add_fusion.4
  979.6 3.2 bitcast_add_fusion.4
  985.3 3.2 bitcast_add_fusion.4
  991.1 3.2 bitcast_add_fusion.4
  996.9 3.2 bitcast_add_fusion.4
  1002.7 3.2 bitcast_add_fusion.4
  1008.4 3.2 bitcast_add_fusion.4
  1014.2 3.2 bitcast_add_fusion.4
  1020.0 3.2 bitcast_add_fusion.4
  1025.8 3.2 bitcast_add_fusion.4
  1031.6 3.2 bitcast_add_fusion.4
  1037.3 3.2 bitcast_add_fusion.4
  1043.1 3.2 bitcast_add_fusion.4
  1048.9 3.2 bitcast_add_fusion.4
  1054.7 3.2 bitcast_add_fusion.4
  1060.4 3.2 bitcast_add_fusion.4
  1063.7 2.2 fusion.51
  (419 shorter events, 110.6 us)
Async XLA Ops:
  7.2 27.8 %copy-start = (bf16[128,1,256]{2,0,1:T(8,128)(2,1)S(1)}, bf16[128,1,256]{2,0,1:T(8,128)(2,1)}, u32[]{:S(2)}) copy-start(bf16[128,1,256]{2,0,1:T(8,128)(2,1)} %param.24) | copy-start | bytes 196612
  7.2 123.2 %all-gather.9.cloned.1.call-start = ((), (), s32[]{:S(2)}) async-start(), calls=%async_computation.4 | async-start | bytes 2162688 | tf_op jit(solution)/shard_map/all_gather | solution.py:62
  10.3 24.3 %all-to-all-start = ((f32[32,1,16]{2,1,0:T(1,128)}), f32[32,1,16]{2,1,0:T(1,128)S(1)}, u32[]{:S(2)}, u32[]{:S(2)}) async-start(f32[32,1,16]{2,1,0:T(1,128)} %broadcast_in_dim.151), calls=%async_computation | async-start | bytes 32768 | tf_op jit(solution)/shard_map/all_to_all | solution.py:26
  15.5 488.2 %all-gather.7.cloned.1.call-start = ((), (), s32[]{:S(2)}) async-start(), calls=%async_computation.3 | async-start | bytes 34603008 | tf_op jit(solution)/shard_map/all_gather | solution.py:205
  35.0 3.3 copy-start.20
  35.0 4.3 copy-start.13
  35.0 4.5 copy-start.8
  35.0 4.6 copy-start.16
  36.6 3.4 copy-start.6
  36.7 4.6 copy-start.10
  36.7 4.6 copy-start.11
  36.7 846.3 %all-gather.5.cloned.1.call-start = ((), (), s32[]{:S(2)}) async-start(), calls=%async_computation.2 | async-start | bytes 34603008 | tf_op jit(solution)/shard_map/all_gather | solution.py:13
  41.3 67.8 %copy-start.9 = (bf16[128,1,256]{2,0,1:T(8,128)(2,1)S(1)}, bf16[128,1,256]{2,0,1:T(8,128)(2,1)}, u32[]{:S(2)}) copy-start(bf16[128,1,256]{2,0,1:T(8,128)(2,1)} %param.25) | copy-start | bytes 196612
  109.1 33.3 %copy-start.17 = (pred[32]{0:T(512)(128)(4,1)}, pred[32]{0:T(512)(128)(4,1)S(1)}, u32[]{:S(2)}) copy-start(pred[32]{0:T(512)(128)(4,1)S(1)} %iota_compare_fusion.4) | copy-start | bytes 100
  132.1 10.0 copy-start.19
  887.1 3.2 copy-start.15
  892.9 3.2 copy-start.15
  898.7 3.2 copy-start.15
  904.5 3.2 copy-start.15
  916.0 3.2 copy-start.15
  921.8 3.2 copy-start.15
  927.6 3.2 copy-start.15
  933.3 3.2 copy-start.15
  939.1 3.2 copy-start.15
  944.9 3.2 copy-start.15
  950.7 3.2 copy-start.15
  956.4 3.2 copy-start.15
  962.2 3.2 copy-start.15
  968.0 3.2 copy-start.15
  973.8 3.2 copy-start.15
  979.5 3.2 copy-start.15
  985.3 3.2 copy-start.15
  991.1 3.2 copy-start.15
  996.9 3.2 copy-start.15
  1002.7 3.2 copy-start.15
  1008.4 3.2 copy-start.15
  1014.2 3.2 copy-start.15
  1025.8 3.2 copy-start.15
  1031.5 3.2 copy-start.15
  1037.3 3.2 copy-start.15
  1043.1 3.2 copy-start.15
  1048.9 3.2 copy-start.15
  1063.7 3.3 copy-start.2
  1063.7 3.3 copy-start.3
  1063.7 3.3 copy-start.4
  1063.7 3.3 copy-start.7
  1063.7 3.3 copy-start.18
  1063.7 4.1 copy-start.1
  (37 other events, 36.2 us)
Sparse Core Ops, SparseCore 0:
  10.7 119.6 all-gather.8
  132.5 371.1 all-gather.6
  505.8 377.1 all-gather.4
